TPU v7x, 32 devices: a whole 2x2x4 slice. The times are simulated.
32 devices in a mesh: rows: 8 (over y, x, core), cols: 4 (over z).
Axes of the slice: x: 2, y: 2, z: 4, core: 2. Of those that a mesh axis runs over, the one named last changes fastest.
Arguments:
- coarse: float32 [512, 512], P('rows', 'cols'), may hold values from -6 to 6
- detail4: float32 [3, 512, 512], P(None, 'rows', 'cols'), may hold values from -6 to 6
- detail3: float32 [3, 1024, 1024], P(None, 'rows', 'cols'), may hold values from -6 to 6
- detail2: float32 [3, 2048, 2048], P(None, 'rows', 'cols'), may hold values from -6 to 6
- detail1: float32 [3, 4096, 4096], P(None, 'rows', 'cols'), may hold values from -6 to 6
Outputs:
- image: float32 [8192, 8192], P('rows', 'cols')
All inputs are finite; a program needn't handle non-finite values.
Results may differ from a plain program's by a relative error of at most 0.00013.
Values sent between devices are 32-bit elements; how exact they have to be, the bound alone decides.
A program may use at most 128 MiB of HBM per device.

v0:
```python
import functools
import math

import jax
import jax.numpy as jnp
from jax import lax
from jax.experimental import pallas as pl
from jax.experimental.pallas import tpu as pltpu
from jax.sharding import PartitionSpec as P

lift_alpha = -1.586134342059924
lift_beta = -0.052980118572961
lift_gamma = 0.882911075530934
lift_delta = 0.443506852043971
lift_scale = 1.149604398860241

MESH = pl.DeviceIdType.MESH
LANES = 128
SUB = 8
UNROLL = 4


def groups_of(height):
    return min(16, height // SUB)


def lanes_of(shape):
    return lax.broadcasted_iota(jnp.int32, shape, len(shape) - 1)


def rows_of(shape):
    return lax.broadcasted_iota(jnp.int32, shape, len(shape) - 2)


def exchange(mesh_shape, levels, *refs):
    count = len(levels)
    inputs, refs = refs[:count], refs[count:]
    below, above, refs = refs[:count], refs[count : 2 * count], refs[2 * count :]
    from_right, from_left, down_right, down_left, up_right, up_left, *refs = refs
    packed, top, bottom, *refs = refs
    firsts, lasts, refs = refs[:count], refs[count : 2 * count], refs[2 * count :]
    local_sem, send_sem, recv_sem = refs

    n_rows, n_cols = mesh_shape
    row, col = lax.axis_index("rows"), lax.axis_index("cols")
    row_next, row_prev = lax.rem(row + 1, n_rows), lax.rem(row + n_rows - 1, n_rows)
    col_next, col_prev = lax.rem(col + 1, n_cols), lax.rem(col + n_cols - 1, n_cols)

    barrier = pltpu.get_barrier_semaphore()
    neighbours = [
        (r, c)
        for r in (row_prev, row, row_next)
        for c in (col_prev, col, col_next)
        if not (r is row and c is col)
    ]
    for place in neighbours:
        pl.semaphore_signal(barrier, inc=1, device_id=place, device_id_type=MESH)

    loads = []
    for i, (bands, height, width) in enumerate(levels):
        for j, (slab, start) in enumerate(((firsts[i], 0), (lasts[i], width - LANES))):
            copy = pltpu.make_async_copy(
                inputs[i].at[:, :, pl.ds(start, LANES)], slab, local_sem.at[2 * i + j]
            )
            copy.start()
            loads.append(copy)

    pl.semaphore_wait(barrier, len(neighbours))

    sends = []

    def send(src, dst, place):
        k = len(sends)
        copy = pltpu.make_async_remote_copy(
            src_ref=src,
            dst_ref=dst,
            send_sem=send_sem.at[k],
            recv_sem=recv_sem.at[k],
            device_id=place,
            device_id_type=MESH,
        )
        copy.start()
        sends.append(copy)

    for i in reversed(range(count)):
        height = levels[i][1]
        send(inputs[i].at[:, pl.ds(0, SUB), :], below[i], (row_prev, col))
        send(inputs[i].at[:, pl.ds(height - SUB, SUB), :], above[i], (row_next, col))

    for copy in loads:
        copy.wait()

    tops = bottoms = None
    offset = place = 0
    for i, (bands, height, width) in enumerate(levels):
        groups = groups_of(height)
        part = height // groups
        lane = lanes_of((part, LANES))
        slot = lax.rem(lane + 4, LANES) // 8
        lane8 = lanes_of((SUB, LANES))
        slot8 = lax.rem(lane8 + 4, LANES) // 8
        for b in range(bands):
            total = None
            for g in range(groups):
                rows = pl.ds(g * part, part)
                edge = jnp.where(lane < 64, firsts[i][b, rows, :], lasts[i][b, rows, :])
                if g:
                    edge = pltpu.roll(edge, 8 * g, 1)
                total = edge if total is None else jnp.where(slot == g, edge, total)
            packed[pl.ds(offset, part), :] = total
            offset += part
            for end in range(2):
                rows = pl.ds(0 if end == 0 else height - SUB, SUB)
                edge = jnp.where(lane8 < 64, firsts[i][b, rows, :], lasts[i][b, rows, :])
                if place:
                    edge = pltpu.roll(edge, 8 * place, 1)
                if end == 0:
                    tops = edge if tops is None else jnp.where(slot8 == place, edge, tops)
                else:
                    bottoms = edge if bottoms is None else jnp.where(slot8 == place, edge, bottoms)
            place += 1
    top[...] = tops
    bottom[...] = bottoms

    send(packed, from_right, (row, col_prev))
    send(packed, from_left, (row, col_next))
    send(top, down_right, (row_prev, col_prev))
    send(top, down_left, (row_prev, col_next))
    send(bottom, up_right, (row_next, col_prev))
    send(bottom, up_left, (row_next, col_next))
    for copy in sends:
        copy.wait()


def lifted(smooth, rough, before, after):
    smooth = smooth - lift_delta * (rough + before(rough))
    rough = rough - lift_gamma * (smooth + after(smooth))
    smooth = smooth - lift_beta * (rough + before(rough))
    rough = rough - lift_alpha * (smooth + after(smooth))
    return smooth, rough


def synthesis(sizes, chunk_rows, piece_rows, *refs):
    count = len(sizes)
    arrays = count + 1
    inputs, refs = refs[:arrays], refs[arrays:]
    below, above, refs = refs[:arrays], refs[arrays : 2 * arrays], refs[2 * arrays :]
    from_right, from_left, down_right, down_left, up_right, up_left, out, *refs = refs
    bands, joined, refs = refs[:count], refs[count], refs[count + 1 :]
    finished, load_sem, store_sem, *stages = refs

    loads = []
    k = 0
    for level, (height, width) in enumerate(sizes):
        mine = []
        for c in range(width // LANES):
            columns = pl.ds(c * LANES, LANES)
            if level == 0:
                copy = pltpu.make_async_copy(
                    inputs[0].at[:, :, columns],
                    bands[0].at[pl.ds(0, 1), c, pl.ds(0, height), :],
                    load_sem.at[k],
                )
                copy.start()
                mine.append(copy)
                k += 1
            copy = pltpu.make_async_copy(
                inputs[level + 1].at[:, :, columns],
                bands[level].at[pl.ds(1, 3), c, pl.ds(0, height), :],
                load_sem.at[k],
            )
            copy.start()
            mine.append(copy)
            k += 1
        loads.append(mine)

    lane = lanes_of((SUB, LANES))
    sub = rows_of((SUB, LANES))
    even = lax.rem(lane, 2) == 0
    low = lane < 64
    pick_low = lane // 2 + jnp.where(even, 0, 64)
    pick_high = lane // 2 + jnp.where(even, 64, 0)
    right_side = lax.rem(lane, 8) < 4

    corner = jnp.where(
        sub < 4,
        jnp.where(right_side, down_right[...], down_left[...]),
        jnp.where(right_side, up_right[...], up_left[...]),
    )
    offset = place = 0
    for i in range(arrays):
        level = max(i - 1, 0)
        height, width = sizes[level]
        groups = groups_of(height)
        part = height // groups
        tiles = width // LANES
        wide = lax.rem(lanes_of((part, LANES)), 8) < 4
        for b in range(1 if i == 0 else 3):
            ref = bands[level].at[b if i == 0 else b + 1]
            rows = pl.ds(offset, part)
            edge = jnp.where(wide, from_right[rows, :], from_left[rows, :])
            for g in range(groups):
                ref[tiles, pl.ds(g * part, part), :] = (
                    pltpu.roll(edge, LANES - 8 * g, 1) if g else edge
                )
            offset += part
            for c in range(tiles):
                columns = pl.ds(c * LANES, LANES)
                ref[c, pl.ds(height, SUB), :] = jnp.where(
                    sub < 4, below[i][b, :, columns], above[i][b, :, columns]
                )
            ref[tiles, pl.ds(height, SUB), :] = (
                pltpu.roll(corner, LANES - 8 * place, 1) if place else corner
            )
            place += 1

    big, small = lift_scale * lift_scale, 1.0 / (lift_scale * lift_scale)

    def vertical(ref, c, start, length, before, after, into):
        def window(b):
            body = ref[b, c, pl.ds(start, length), :]
            halo = jnp.where(
                sub < 4, ref[b, c, pl.ds(after, SUB), :], ref[b, c, pl.ds(before, SUB), :]
            )
            return jnp.concatenate([body, halo], axis=0)

        total = length + SUB
        shift_down = lambda x: pltpu.roll(x, 1, 0)
        shift_up = lambda x: pltpu.roll(x, total - 1, 0)
        for half, (s, r) in enumerate(((0, 2), (1, 3))):
            smooth, rough = window(s), window(r)
            if half == 0:
                smooth = smooth * big
            else:
                rough = rough * small
            smooth, rough = lifted(smooth, rough, shift_down, shift_up)
            joined[half, c, pl.ds(into, length, stride=2), :] = smooth[:length]
            joined[half, c, pl.ds(into + 1, length, stride=2), :] = rough[:length]

    def rolled_before(x, n):
        turned = [pltpu.roll(t, 1, 1) for t in x]
        return [jnp.where(lane == 0, turned[c - 1], turned[c]) for c in range(n)]

    def rolled_after(x, n):
        turned = [pltpu.roll(t, LANES - 1, 1) for t in x]
        return [jnp.where(lane == LANES - 1, turned[(c + 1) % n], turned[c]) for c in range(n)]

    def step(x, factor, y, z):
        return [a - factor * (b + c) for a, b, c in zip(x, y, z)]

    def interleave(smooth, rough, tiles, store, last):
        for c in range(tiles if last else tiles + 1):
            first = jnp.where(low, smooth[c], rough[c])
            second = jnp.where(low, rough[c], smooth[c])
            first = jnp.take_along_axis(first, pick_low, axis=1, mode="promise_in_bounds")
            second = jnp.take_along_axis(second, pick_high, axis=1, mode="promise_in_bounds")
            left = jnp.where(even, first, second)
            right = jnp.where(even, second, first)
            if c < tiles:
                store(2 * c, left)
                store(2 * c + 1, right)
            else:
                store(2 * c, jnp.where(low, left, right))

    def horizontal(tiles, load, store, last):
        n = tiles + 1
        smooth = [load(0, c) for c in range(n)]
        rough = [load(1, c) for c in range(n)]
        smooth = step(smooth, lift_delta, rough, rolled_before(rough, n))
        rough = step(rough, lift_gamma, smooth, rolled_after(smooth, n))
        smooth = step(smooth, lift_beta, rough, rolled_before(rough, n))
        rough = step(rough, lift_alpha, smooth, rolled_after(smooth, n))
        interleave(smooth, rough, tiles, store, last)

    def pipelined(tiles, total, unroll, target, last, after_step):
        n = tiles + 1
        s1, r1, s2, r2 = stages
        groups = total // (SUB * unroll)

        def body(t, carry):
            def rows_at(group, u):
                first = jnp.clip(group, 0, groups - 1) * (SUB * unroll) + u * SUB
                return pl.ds(pl.multiple_of(first, SUB), SUB)

            def get(buffer, group, u):
                slot = lax.rem(group + 8, 2)
                return [buffer[slot, u, c] for c in range(n)]

            def put(buffer, group, u, value):
                slot = lax.rem(group + 8, 2)
                for c in range(n):
                    buffer[slot, u, c] = value[c]

            for u in range(unroll):
                into = rows_at(t - 4, u)

                def store(c, value, into=into):
                    target[c, into, :] = value

                interleave(get(s2, t - 4, u), get(r2, t - 4, u), tiles, store, last)
            for u in range(unroll):
                smooth = get(s2, t - 3, u)
                put(r2, t - 3, u, step(get(r1, t - 3, u), lift_alpha, smooth, rolled_after(smooth, n)))
            for u in range(unroll):
                rough = get(r1, t - 2, u)
                put(s2, t - 2, u, step(get(s1, t - 2, u), lift_beta, rough, rolled_before(rough, n)))
            for u in range(unroll):
                smooth = get(s1, t - 1, u)
                rough = [joined[1, c, rows_at(t - 1, u), :] for c in range(n)]
                put(r1, t - 1, u, step(rough, lift_gamma, smooth, rolled_after(smooth, n)))
            for u in range(unroll):
                smooth = [joined[0, c, rows_at(t, u), :] for c in range(n)]
                rough = [joined[1, c, rows_at(t, u), :] for c in range(n)]
                put(s1, t, u, step(smooth, lift_delta, rough, rolled_before(rough, n)))
            after_step(t - 4, groups)
            return carry

        lax.fori_loop(0, groups + 4, body, 0)

    for level, (height, width) in enumerate(sizes):
        tiles = width // LANES
        last = level == count - 1
        rows = min(chunk_rows, height)
        chunks = height // rows
        unroll = math.gcd(max(UNROLL, 16 // tiles), 2 * rows // SUB)
        ref = bands[level]
        target = finished if last else bands[level + 1].at[0]
        for copy in loads[level]:
            copy.wait()

        def one_chunk(i, carry):
            start = pl.multiple_of(i * rows, SUB)
            before = pl.multiple_of(jnp.where(i == 0, height, start - SUB), SUB)
            after = pl.multiple_of(start + rows, SUB)
            into = pl.multiple_of(2 * start, SUB)

            def one_column(c, carry):
                vertical(ref, c, start, rows, before, after, into)
                return carry

            lax.fori_loop(0, tiles + 1, one_column, 0)
            return carry

        lax.fori_loop(0, chunks, one_chunk, 0)

        def store_copy(piece, c):
            span = pl.ds(pl.multiple_of(piece * piece_rows, SUB), piece_rows)
            return pltpu.make_async_copy(
                finished.at[c, span, :],
                out.at[span, pl.ds(c * LANES, LANES)],
                store_sem.at[piece, c],
            )

        if tiles >= 4:
            unroll = UNROLL if last else 2 * UNROLL

            def after_step(group, groups):
                if not last:
                    return
                every = piece_rows // (SUB * unroll)

                @pl.when((group >= 0) & (lax.rem(group + every, every) == every - 1))
                def _():
                    for c in range(2 * tiles):
                        store_copy(group // every, c).start()

            pipelined(tiles, 2 * height, unroll, target, last, after_step)
        else:
            unroll = math.gcd(16, 2 * height // SUB)

            def one_row(t, carry):
                for u in range(unroll):
                    where = pl.ds(pl.multiple_of((t * unroll + u) * SUB, SUB), SUB)

                    def store(c, value, where=where):
                        target[c, where, :] = value

                    def load(half, c, where=where):
                        return joined[half, c, where, :]

                    horizontal(tiles, load, store, last)
                return carry

            lax.fori_loop(0, 2 * height // (SUB * unroll), one_row, 0)

        if not last:

            def edge_column(c, carry):
                vertical(ref, c, height, SUB, height - SUB, 0, 0)
                return carry

            lax.fori_loop(0, tiles + 1, edge_column, 0)

            def load(half, c):
                return jnp.where(
                    sub < 4, joined[half, c, pl.ds(0, SUB), :], joined[half, c, pl.ds(SUB, SUB), :]
                )

            def store(c, value):
                target[c, pl.ds(2 * height, SUB), :] = value

            horizontal(tiles, load, store, False)
        else:
            for piece in range(2 * height // piece_rows):
                for c in range(2 * tiles):
                    store_copy(piece, c).wait()


def per_device(mesh_shape, coarse, *details):
    arrays = (coarse[None],) + details
    levels = [a.shape for a in arrays]
    sizes = [d.shape[1:] for d in details]
    f32 = jnp.float32
    shape = lambda *dims: jax.ShapeDtypeStruct(dims, f32)
    packed_rows = sum(b * (h // groups_of(h)) for b, h, w in levels)
    strips = [shape(b, SUB, w) for b, h, w in levels]
    anywhere = pl.BlockSpec(memory_space=pl.ANY)
    in_vmem = pl.BlockSpec(memory_space=pltpu.VMEM)
    n = len(levels)
    halo_shapes = strips + strips + [shape(packed_rows, LANES)] * 2 + [shape(SUB, LANES)] * 4
    n_sends = 2 * n + 6
    halos = pl.pallas_call(
        functools.partial(exchange, mesh_shape, levels),
        out_shape=halo_shapes,
        in_specs=[anywhere] * n,
        out_specs=[anywhere] * len(halo_shapes),
        scratch_shapes=[
            pltpu.VMEM((packed_rows, LANES), f32),
            pltpu.VMEM((SUB, LANES), f32),
            pltpu.VMEM((SUB, LANES), f32),
        ]
        + [pltpu.VMEM((b, h, LANES), f32) for b, h, w in levels] * 2
        + [
            pltpu.SemaphoreType.DMA((2 * n,)),
            pltpu.SemaphoreType.DMA((n_sends,)),
            pltpu.SemaphoreType.DMA((n_sends,)),
        ],
        compiler_params=pltpu.CompilerParams(collective_id=0, has_side_effects=True),
        name="exchange",
    )(*arrays)

    chunk_rows = 64
    height, width = sizes[-1]
    n_loads = sum(w // LANES for h, w in sizes) + sizes[0][1] // LANES
    piece_rows = math.gcd(128, 2 * height)
    return pl.pallas_call(
        functools.partial(synthesis, sizes, chunk_rows, piece_rows),
        out_shape=shape(2 * height, 2 * width),
        in_specs=[anywhere] * n + [in_vmem] * len(halo_shapes),
        out_specs=anywhere,
        scratch_shapes=[
            pltpu.VMEM((4, w // LANES + 1, h + SUB, LANES), f32) for h, w in sizes
        ]
        + [
            pltpu.VMEM((2, width // LANES + 1, 2 * height, LANES), f32),
            pltpu.VMEM((2 * width // LANES, 2 * height, LANES), f32),
            pltpu.SemaphoreType.DMA((n_loads,)),
            pltpu.SemaphoreType.DMA((2 * height // piece_rows, 2 * width // LANES)),
        ]
        + [pltpu.VMEM((2, 2 * UNROLL, width // LANES + 1, SUB, LANES), f32)] * 4,
        compiler_params=pltpu.CompilerParams(vmem_limit_bytes=56 * 1024 * 1024),
        name="synthesis",
    )(*arrays, *halos)


def solution(mesh):
    mesh_shape = (mesh.shape["rows"], mesh.shape["cols"])
    return jax.shard_map(
        functools.partial(per_device, mesh_shape),
        mesh=mesh,
        in_specs=(
            P("rows", "cols"),
            P(None, "rows", "cols"),
            P(None, "rows", "cols"),
            P(None, "rows", "cols"),
            P(None, "rows", "cols"),
        ),
        out_specs=P("rows", "cols"),
        check_vma=False,
    )
```

profile of v0, /device:TPU:0, one launch (start us, length us, event | category | flops | bytes accessed | tf_op | source)
XLA Modules:
  0.0 42.2 jit_solution(2785731367741407209)
XLA Ops:
  0.0 14.4 %exchange.1 = (f32[1,8,128]{2,1,0:T(8,128)}, f32[3,8,128]{2,1,0:T(8,128)}, f32[3,8,256]{2,1,0:T(8,128)}, f32[3,8,512]{2,1,0:T(8,128)}, f32[3,8,1024]{2,1,0:T(8,1...) custom-call(f32[1,64,128]{2,1,0:T(8,128)} %bitcast.1, ...), custom_call_target="tpu_custom_call" | custom-call | tf_op jit(solution)/shard_map/exchange/pallas_call | solution.py:422
  14.4 27.8 %synthesis.1 = f32[1024,2048]{1,0:T(8,128)} custom-call(f32[1,64,128]{2,1,0:T(8,128)} %bitcast.2, f32[3,64,128]{2,1,0:T(8,128)} %refs_1_.3, f32[3,128,256]{2,1,0:T(8,128)} %refs_2_.3, f32[3,256,512]{2,1,0:T(8,128)} %refs_3_.3, f32[3,512,1024]{2,1,0:T(8,128)} %refs_4_.3, f32[1,8,128]{2,1,0:T(8,128)} %get-tuple-element.21.refs_5_, ...), custom_call_target="tpu_custom_call" | custom-call | tf_op jit(solution)/shard_map/synthesis/pallas_call | solution.py:446
where the time goes:
time: 42.4 us; the launch traced here: 42.2 us
  Pallas kernels  42.2 us (100%)
    pallas_call x1, Pallas kernels, per_device(): pl.pallas_call(functools.partial(synthesis, sizes, chunk_rows, piece_rows...  27.8 us
    pallas_call x1, Pallas kernels, per_device(): pl.pallas_call(functools.partial(exchange, mesh_shape, levels), out_shape...  14.4 us

commit v1 on v0

v1 whole, which is shorter than its diff:
```python
import functools

import jax
import jax.numpy as jnp
from jax import lax
from jax.experimental import pallas as pl
from jax.experimental.pallas import tpu as pltpu
from jax.sharding import PartitionSpec as P

lift_alpha = -1.586134342059924
lift_beta = -0.052980118572961
lift_gamma = 0.882911075530934
lift_delta = 0.443506852043971
lift_scale = 1.149604398860241

MESH = pl.DeviceIdType.MESH
LANES = 128
SUB = 8
BIG, SMALL = lift_scale * lift_scale, 1.0 / (lift_scale * lift_scale)


def lanes_of(shape):
    return lax.broadcasted_iota(jnp.int32, shape, len(shape) - 1)


def rows_of(shape):
    return lax.broadcasted_iota(jnp.int32, shape, len(shape) - 2)


def eight(start):
    return pl.ds(pl.multiple_of(start, SUB), SUB)


def block(start):
    return pl.ds(pl.multiple_of(start, SUB), LANES)


def lift(get_smooth, get_rough, put_even, put_odd, steps):
    before = get_rough(-1)
    smooth = get_smooth(-1) - lift_delta * (before + get_rough(-2))
    r0 = get_rough(0)
    s1 = get_smooth(0) - lift_delta * (r0 + before)
    r2_before = before - lift_gamma * (smooth + s1)
    r0_next = get_rough(1)
    s1_next = get_smooth(1) - lift_delta * (r0_next + r0)
    r2 = r0 - lift_gamma * (s1 + s1_next)
    s3 = s1 - lift_beta * (r2 + r2_before)
    s1, r0 = s1_next, r0_next
    for v in range(steps):
        r0_next = get_rough(v + 2)
        s1_next = get_smooth(v + 2) - lift_delta * (r0_next + r0)
        r2_next = r0 - lift_gamma * (s1 + s1_next)
        s3_next = s1 - lift_beta * (r2_next + r2)
        put_even(v, s3)
        put_odd(v, r2 - lift_alpha * (s3 + s3_next))
        s1, r0, r2, s3 = s1_next, r0_next, r2_next, s3_next


def vertical(smooth_ref, rough_ref, out_ref, height, half):
    steps = (height + SUB) // SUB

    def smooth(v):
        x = smooth_ref[pl.ds(4 + v, SUB, stride=steps), :]
        return x * BIG if half == 0 else x

    def rough(v):
        x = rough_ref[pl.ds(4 + v, SUB, stride=steps), :]
        return x * SMALL if half == 1 else x

    def even(v, x):
        out_ref[pl.ds(2 * v, SUB, stride=2 * steps), :] = x

    def odd(v, x):
        out_ref[pl.ds(2 * v + 1, SUB, stride=2 * steps), :] = x

    lift(smooth, rough, even, odd, steps)


def horizontal(turned, spread, width, wrap):
    steps = (width + SUB) // SUB

    def smooth(v):
        return turned[0, pl.ds(4 + v, SUB, stride=steps), :]

    def rough(v):
        return turned[1, pl.ds(4 + v, SUB, stride=steps), :]

    def even(v, x):
        spread[pl.ds(2 * v, SUB, stride=2 * steps), :] = x

    def odd(v, x):
        spread[pl.ds(2 * v + 1, SUB, stride=2 * steps), :] = x

    lift(smooth, rough, even, odd, steps)
    if wrap:
        spread[pl.ds(SUB + 2 * width + LANES - SUB, SUB), :] = spread[pl.ds(0, SUB), :]


def turn_in(joined, turned, k, tiles):
    for half in range(2):
        for c in range(tiles + 1):
            turned[half, pl.ds(SUB + LANES * c, LANES), :] = joined[
                half, c, block(SUB + LANES * k), :
            ].T
        turned[half, pl.ds(0, SUB), :] = turned[
            half, pl.ds(SUB + LANES * tiles + LANES - SUB, SUB), :
        ]


def blocks_of(count, tin, across, tout, turned, spread):
    tin(0, turned[0])
    across(turned[0], spread[0])
    if count > 1:
        tin(1, turned[1])
    pairs = (count - 1) // 2

    def two(m, carry):
        k = 2 * m
        tout(k, spread[0])
        across(turned[1], spread[1])
        tin(k + 2, turned[0])
        tout(k + 1, spread[1])
        across(turned[0], spread[0])
        tin(jnp.minimum(k + 3, count - 1), turned[1])
        return carry

    if pairs:
        lax.fori_loop(0, pairs, two, 0)
    if count % 2:
        tout(count - 1, spread[0])
    else:
        tout(count - 2, spread[0])
        across(turned[1], spread[1])
        tout(count - 1, spread[1])


def row_items(levels):
    return [(a, b, c) for a, (n, h, w) in enumerate(levels) for b in range(n) for c in range(w // LANES)]


def column_blocks(levels):
    blocks, short = [], []
    for a, (n, h, w) in enumerate(levels):
        for b in range(n):
            if h < LANES:
                short.append((a, b, 0, h))
                if sum(p[3] for p in short) == LANES:
                    blocks.append(short)
                    short = []
            else:
                blocks.extend([[(a, b, LANES * k, LANES)] for k in range(h // LANES)])
    return blocks + ([short] if short else [])


def coarse_levels(mesh_shape, levels, *refs):
    count = len(levels)
    inputs, refs = refs[:count], refs[count:]
    low_out, detail_out, refs = refs[0], refs[1], refs[2:]
    lows, refs = list(refs[: count - 2]) + [low_out], refs[count - 2 :]
    details, refs = list(refs[: count - 2]) + [detail_out], refs[count - 2 :]
    tops, bottoms, refs = refs[:count], refs[count : 2 * count], refs[2 * count :]
    joined, turned_a, turned_b, spread_a, spread_b, *refs = refs
    send_top, send_bottom, below, above, *refs = refs
    send_first, send_last, from_right, from_left, *refs = refs
    corner_top, corner_bottom, down_right, down_left, up_right, up_left, *refs = refs
    edge_sem, body_sem, send_sem, recv_sem = refs

    def band(a, b):
        return lows[0] if a == 0 else details[a - 1].at[b]

    n_rows, n_cols = mesh_shape
    row, col = lax.axis_index("rows"), lax.axis_index("cols")
    row_next, row_prev = lax.rem(row + 1, n_rows), lax.rem(row + n_rows - 1, n_rows)
    col_next, col_prev = lax.rem(col + 1, n_cols), lax.rem(col + n_cols - 1, n_cols)

    barrier = pltpu.get_barrier_semaphore()
    neighbours = [
        (r, c)
        for r in (row_prev, row, row_next)
        for c in (col_prev, col, col_next)
        if not (r is row and c is col)
    ]
    for place in neighbours:
        pl.semaphore_signal(barrier, inc=1, device_id=place, device_id_type=MESH)

    edges, bodies = [], []

    def load(src, dst, sem, into):
        copy = pltpu.make_async_copy(src, dst, sem.at[len(into)])
        copy.start()
        into.append(copy)

    def load_tile(a, c, sem, into):
        n, h, w = levels[a]
        src = inputs[a].at[:, :, pl.ds(c * LANES, LANES)]
        if a == 0:
            dst = lows[0].at[pl.ds(c, 1), pl.ds(SUB, h), :]
        else:
            dst = details[a - 1].at[:, c, pl.ds(SUB, h), :]
        load(src, dst, sem, into)

    for a in reversed(range(count)):
        n, h, w = levels[a]
        load(inputs[a].at[:, pl.ds(0, SUB), :], tops[a], edge_sem, edges)
        load(inputs[a].at[:, pl.ds(h - SUB, SUB), :], bottoms[a], edge_sem, edges)
        for c in sorted({0, w // LANES - 1}):
            load_tile(a, c, edge_sem, edges)
    for a in range(count):
        for c in range(1, levels[a][2] // LANES - 1):
            load_tile(a, c, body_sem, bodies)

    lane = lanes_of((SUB, LANES))
    sub = rows_of((SUB, LANES))
    upper = sub < 4

    for copy in edges:
        copy.wait()

    items = row_items(levels)
    for k in range((len(items) + 1) // 2):
        pair = items[2 * k : 2 * k + 2]
        top, bottom = [
            [ref[a][b, :, pl.ds(c * LANES, LANES)] for a, b, c in pair] for ref in (tops, bottoms)
        ]
        top, bottom = [x if len(x) == 2 else x * 2 for x in (top, bottom)]
        send_top[k] = jnp.where(upper, top[0], pltpu.roll(top[1], 4, 0))
        send_bottom[k] = jnp.where(upper, pltpu.roll(bottom[1], 4, 0), bottom[0])

    corner_items = [(a, b) for a in range(count) for b in range(levels[a][0])]
    slot = lax.rem(lane + 4, LANES) // 8
    for ref, out in ((tops, corner_top), (bottoms, corner_bottom)):
        total = None
        for p, (a, b) in enumerate(corner_items):
            w = levels[a][2]
            edge = jnp.where(
                lane < 64, ref[a][b, :, pl.ds(0, LANES)], ref[a][b, :, pl.ds(w - LANES, LANES)]
            )
            if p:
                edge = pltpu.roll(edge, 8 * p, 1)
            total = edge if total is None else jnp.where(slot == p, edge, total)
        out[...] = total

    pl.semaphore_wait(barrier, len(neighbours))

    sends = []

    def send(src, dst, place):
        k = len(sends)
        copy = pltpu.make_async_remote_copy(
            src_ref=src,
            dst_ref=dst,
            send_sem=send_sem.at[k],
            recv_sem=recv_sem.at[k],
            device_id=place,
            device_id_type=MESH,
        )
        copy.start()
        sends.append(copy)

    send(send_top, below, (row_prev, col))
    send(send_bottom, above, (row_next, col))
    send(corner_top, down_right, (row_prev, col_prev))
    send(corner_top, down_left, (row_prev, col_next))
    send(corner_bottom, up_right, (row_next, col_prev))
    send(corner_bottom, up_left, (row_next, col_next))

    blocks = column_blocks(levels)
    first_half = lanes_of((LANES, LANES)) < 64
    turned = []
    for parts in blocks:
        pieces = []
        for a, b, start, length in parts:
            w = levels[a][2]
            rows = pl.ds(SUB + start, length)
            pieces.append(
                jnp.where(
                    first_half[:length],
                    band(a, b)[0, rows, :],
                    band(a, b)[w // LANES - 1, rows, :],
                )
            )
        missing = LANES - sum(p[3] for p in parts)
        if missing:
            pieces.append(jnp.zeros((missing, LANES), jnp.float32))
        whole = pieces[0] if len(pieces) == 1 else jnp.concatenate(pieces, axis=0)
        whole = whole.T
        turned.append((whole[:SUB], whole[LANES - SUB :]))
    for k in range((len(blocks) + 1) // 2):
        one = turned[2 * k]
        two = turned[min(2 * k + 1, len(blocks) - 1)]
        send_first[k] = jnp.where(upper, one[0], pltpu.roll(two[0], 4, 0))
        send_last[k] = jnp.where(upper, pltpu.roll(two[1], 4, 0), one[1])
    send(send_first, from_right, (row, col_prev))
    send(send_last, from_left, (row, col_next))

    for copy in bodies:
        copy.wait()
    for copy in sends:
        copy.wait()

    for k in range((len(items) + 1) // 2):
        for i, (a, b, c) in enumerate(items[2 * k : 2 * k + 2]):
            h = levels[a][1]
            after, before = below[k], above[k]
            if i:
                after, before = pltpu.roll(after, 4, 0), pltpu.roll(before, 4, 0)
            band(a, b)[c, pl.ds(SUB + h, SUB), :] = after
            band(a, b)[c, pl.ds(0, SUB), :] = before
    for k in range((len(blocks) + 1) // 2):
        for i, parts in enumerate(blocks[2 * k : 2 * k + 2]):
            after, before = from_right[k], from_left[k]
            if i:
                after, before = pltpu.roll(after, 4, 0), pltpu.roll(before, 4, 0)
            whole = jnp.concatenate(
                [after, jnp.zeros((LANES - 2 * SUB, LANES), jnp.float32), before], axis=0
            ).T
            place = 0
            for a, b, start, length in parts:
                band(a, b)[levels[a][2] // LANES, pl.ds(SUB + start, length), :] = whole[
                    place : place + length
                ]
                place += length
    right_side = lax.rem(lane, 8) < 4
    corner = jnp.where(
        upper,
        jnp.where(right_side, down_right[...], down_left[...]),
        jnp.where(right_side, up_right[...], up_left[...]),
    )
    for p, (a, b) in enumerate(corner_items):
        n, h, w = levels[a]
        here = pltpu.roll(corner, LANES - 8 * p, 1) if p else corner
        band(a, b)[w // LANES, pl.ds(0, SUB), :] = here
        band(a, b)[w // LANES, pl.ds(SUB + h, SUB), :] = here

    for level in range(count - 2):
        n, h, w = levels[level + 1]
        tiles = w // LANES
        low, detail, target = lows[level], details[level], lows[level + 1]

        def columns(c, carry):
            for half in range(2):
                smooth = low.at[c] if half == 0 else detail.at[0, c]
                rough = detail.at[1, c] if half == 0 else detail.at[2, c]
                out = joined.at[half, c]
                vertical(smooth, rough, out, h, half)
                out[pl.ds(SUB + 2 * h + LANES - SUB, SUB), :] = out[pl.ds(0, SUB), :]
            return carry

        lax.fori_loop(0, tiles + 1, columns, 0)

        def tin(k, turned):
            turn_in(joined, turned, k, tiles)

        def across(turned, spread):
            horizontal(turned, spread, w, True)

        def tout(k, spread):
            for j in range(2 * tiles + 1):
                target[j, block(SUB + LANES * k), :] = spread[pl.ds(SUB + LANES * j, LANES), :].T

        blocks_of(2 * h // LANES + 1, tin, across, tout, (turned_a, turned_b), (spread_a, spread_b))
        for j in range(2 * tiles + 1):
            target[j, pl.ds(0, SUB), :] = target[j, pl.ds(SUB + 2 * h + LANES - SUB, SUB), :]


def finest_level(height, width, low, detail, out, joined, *refs):
    turned_a, turned_b, spread_a, spread_b, finished, store_sem = refs
    tiles = width // LANES

    def columns(c, carry):
        for half in range(2):
            smooth = low.at[c] if half == 0 else detail.at[0, c]
            rough = detail.at[1, c] if half == 0 else detail.at[2, c]
            vertical(smooth, rough, joined.at[half, c], height, half)
        return carry

    lax.fori_loop(0, tiles + 1, columns, 0)

    def store_copy(k, j):
        rows = block(LANES * k)
        return pltpu.make_async_copy(
            finished.at[j, rows, :], out.at[rows, pl.ds(j * LANES, LANES)], store_sem.at[k, j]
        )

    def tin(k, turned):
        turn_in(joined, turned, k, tiles)

    def across(turned, spread):
        horizontal(turned, spread, width, False)

    def tout(k, spread):
        for j in range(2 * tiles):
            finished[j, block(LANES * k), :] = spread[pl.ds(SUB + LANES * j, LANES), :].T
            store_copy(k, j).start()

    count = 2 * height // LANES
    blocks_of(count, tin, across, tout, (turned_a, turned_b), (spread_a, spread_b))
    for k in range(count):
        for j in range(2 * tiles):
            store_copy(k, j).wait()


def per_device(mesh_shape, coarse, *details):
    arrays = (coarse[None],) + details
    arrays = tuple(pltpu.with_memory_space_constraint(a, pltpu.HBM) for a in arrays)
    levels = [a.shape for a in arrays]
    count = len(levels)
    f32 = jnp.float32
    vmem = lambda *dims: pltpu.VMEM(dims, f32)
    anywhere = pl.BlockSpec(memory_space=pl.ANY)
    in_vmem = pl.BlockSpec(memory_space=pltpu.VMEM)
    n_pairs = (len(row_items(levels)) + 1) // 2
    n_blocks = (len(column_blocks(levels)) + 1) // 2
    n_edges = sum(2 + len({0, w // LANES - 1}) for n, h, w in levels)
    n_bodies = sum(max(w // LANES - 2, 0) for n, h, w in levels)
    n, h, w = levels[-2]
    low_shape = lambda h, w: (w // LANES + 1, SUB + h + LANES, LANES)
    detail_shape = lambda h, w: (3, w // LANES + 1, h + 2 * SUB, LANES)
    _, height, width = levels[-1]
    low, detail = pl.pallas_call(
        functools.partial(coarse_levels, mesh_shape, levels),
        out_shape=[vmem(*low_shape(height, width)), vmem(*detail_shape(height, width))],
        in_specs=[anywhere] * count,
        out_specs=[in_vmem] * 2,
        scratch_shapes=[vmem(*low_shape(h, w)) for _, h, w in levels[1:-1]]
        + [vmem(*detail_shape(h, w)) for _, h, w in levels[1:-1]]
        + [vmem(b, SUB, w) for b, h, w in levels] * 2
        + [vmem(2, w // LANES + 1, SUB + 2 * h + LANES, LANES)]
        + [vmem(2, SUB + w + LANES, LANES)] * 2
        + [vmem(SUB + 2 * w + LANES, LANES)] * 2
        + [vmem(n_pairs, SUB, LANES)] * 4
        + [vmem(n_blocks, SUB, LANES)] * 4
        + [vmem(SUB, LANES)] * 6
        + [
            pltpu.SemaphoreType.DMA((n_edges,)),
            pltpu.SemaphoreType.DMA((max(n_bodies, 1),)),
            pltpu.SemaphoreType.DMA((8,)),
            pltpu.SemaphoreType.DMA((8,)),
        ],
        compiler_params=pltpu.CompilerParams(
            collective_id=0, has_side_effects=True, vmem_limit_bytes=40 * 1024 * 1024
        ),
        name="coarse_levels",
    )(*arrays)

    tiles = width // LANES
    return pl.pallas_call(
        functools.partial(finest_level, height, width),
        out_shape=jax.ShapeDtypeStruct((2 * height, 2 * width), f32),
        in_specs=[in_vmem] * 2,
        out_specs=anywhere,
        scratch_shapes=[vmem(2, tiles + 1, 2 * height + 2 * SUB, LANES)]
        + [vmem(2, SUB + width + LANES, LANES)] * 2
        + [vmem(2 * width + 2 * SUB, LANES)] * 2
        + [
            vmem(2 * tiles, 2 * height, LANES),
            pltpu.SemaphoreType.DMA((2 * height // LANES, 2 * tiles)),
        ],
        compiler_params=pltpu.CompilerParams(vmem_limit_bytes=40 * 1024 * 1024),
        name="finest_level",
    )(low, detail)


def solution(mesh):
    mesh_shape = (mesh.shape["rows"], mesh.shape["cols"])
    return jax.shard_map(
        functools.partial(per_device, mesh_shape),
        mesh=mesh,
        in_specs=(
            P("rows", "cols"),
            P(None, "rows", "cols"),
            P(None, "rows", "cols"),
            P(None, "rows", "cols"),
            P(None, "rows", "cols"),
        ),
        out_specs=P("rows", "cols"),
        check_vma=False,
    )
```

time: 42.4 us -> 26.6 us (0.63)
  Pallas kernels: 42.2 us -> 26.5 us
    pallas_call x2, Pallas kernels: 42.2 us -> 26.5 us  [the longest x1 16.7 us: per_device(): pl.pallas_call(functools.partial(coarse_levels, mesh_shape, levels), out_...]
where the time goes in v1:
time: 26.6 us; the launch traced here: 26.5 us
  Pallas kernels  26.5 us (100%)
    pallas_call x1, Pallas kernels, per_device(): pl.pallas_call(functools.partial(coarse_levels, mesh_shape, levels), out_...  16.7 us
    pallas_call x1, Pallas kernels, per_device(): pl.pallas_call(functools.partial(finest_level, height, width), out_shape=...  9.81 us

profile of v1, /device:TPU:0, one launch (start us, length us, event | category | flops | bytes accessed | tf_op | source)
XLA Modules:
  0.0 26.5 jit_solution(2329471013643792775)
XLA Ops:
  0.0 16.7 %coarse_levels.1 = (f32[9,648,128]{2,1,0:T(8,128)S(1)}, f32[3,9,528,128]{3,2,1,0:T(8,128)S(1)}) custom-call(f32[1,64,128]{2,1,0:T(8,128)} %bitcast.1, f32[3,64,128]{2,1,0:T(8,128)} %refs_1_.1, f32[3,128,256]{2,1,0:T(8,128)} %refs_2_.1, f32[3,256,512]{2,1,0:T(8,128)} %refs_3_.1, f32[3,512,1024]{2,1,0:T(8,128)} %refs_4_.1), custom_call_target="tpu_custom_call" | custom-call | tf_op jit(solution)/shard_map/coarse_levels/pallas_call | solution.py:420
  16.7 9.8 %finest_level.1 = f32[1024,2048]{1,0:T(8,128)} custom-call(f32[9,648,128]{2,1,0:T(8,128)S(1)} %get-tuple-element.7.low, f32[3,9,528,128]{3,2,1,0:T(8,128)S(1)} %get-tuple-element.8.detail), custom_call_target="tpu_custom_call" | custom-call | tf_op jit(solution)/shard_map/finest_level/pallas_call | solution.py:447

commit v2 on v1

--- a/solution.py
+++ b/solution.py
@@ -16,6 +16,7 @@
 MESH = pl.DeviceIdType.MESH
 LANES = 128
 SUB = 8
+STRIP = 72
 BIG, SMALL = lift_scale * lift_scale, 1.0 / (lift_scale * lift_scale)
 
 
@@ -56,15 +57,13 @@
         s1, r0, r2, s3 = s1_next, r0_next, r2_next, s3_next
 
 
-def vertical(smooth_ref, rough_ref, out_ref, height, half):
-    steps = (height + SUB) // SUB
-
+def vertical(smooth_ref, rough_ref, out_ref, steps, half, first=4):
     def smooth(v):
-        x = smooth_ref[pl.ds(4 + v, SUB, stride=steps), :]
+        x = smooth_ref[pl.ds(first + v, SUB, stride=steps), :]
         return x * BIG if half == 0 else x
 
     def rough(v):
-        x = rough_ref[pl.ds(4 + v, SUB, stride=steps), :]
+        x = rough_ref[pl.ds(first + v, SUB, stride=steps), :]
         return x * SMALL if half == 1 else x
 
     def even(v, x):
@@ -76,14 +75,14 @@
     lift(smooth, rough, even, odd, steps)
 
 
-def horizontal(turned, spread, width, wrap):
+def horizontal(smooth_ref, rough_ref, spread, width, wrap):
     steps = (width + SUB) // SUB
 
     def smooth(v):
-        return turned[0, pl.ds(4 + v, SUB, stride=steps), :]
+        return smooth_ref[pl.ds(4 + v, SUB, stride=steps), :]
 
     def rough(v):
-        return turned[1, pl.ds(4 + v, SUB, stride=steps), :]
+        return rough_ref[pl.ds(4 + v, SUB, stride=steps), :]
 
     def even(v, x):
         spread[pl.ds(2 * v, SUB, stride=2 * steps), :] = x
@@ -97,41 +96,48 @@
 
 
 def turn_in(joined, turned, k, tiles):
-    for half in range(2):
-        for c in range(tiles + 1):
-            turned[half, pl.ds(SUB + LANES * c, LANES), :] = joined[
-                half, c, block(SUB + LANES * k), :
-            ].T
-        turned[half, pl.ds(0, SUB), :] = turned[
-            half, pl.ds(SUB + LANES * tiles + LANES - SUB, SUB), :
-        ]
-
-
-def blocks_of(count, tin, across, tout, turned, spread):
-    tin(0, turned[0])
-    across(turned[0], spread[0])
+    for c in range(tiles + 1):
+        turned[pl.ds(SUB + LANES * c, LANES), :] = joined[c, block(SUB + LANES * k), :].T
+    wrap_around(turned, tiles)
+
+
+def wrap_around(turned, tiles):
+    turned[pl.ds(0, SUB), :] = turned[pl.ds(SUB + LANES * tiles + LANES - SUB, SUB), :]
+
+
+def blocks_of(count, tin, across, tout):
+    tin(0, 0)
+    across(0, 0)
     if count > 1:
-        tin(1, turned[1])
+        tin(1, 1)
     pairs = (count - 1) // 2
 
     def two(m, carry):
         k = 2 * m
-        tout(k, spread[0])
-        across(turned[1], spread[1])
-        tin(k + 2, turned[0])
-        tout(k + 1, spread[1])
-        across(turned[0], spread[0])
-        tin(jnp.minimum(k + 3, count - 1), turned[1])
+        tout(k, 0)
+        across(k + 1, 1)
+        tin(k + 2, 0)
+        tout(k + 1, 1)
+        across(k + 2, 0)
+        tin(jnp.minimum(k + 3, count - 1), 1)
         return carry
 
     if pairs:
         lax.fori_loop(0, pairs, two, 0)
     if count % 2:
-        tout(count - 1, spread[0])
+        tout(count - 1, 0)
     else:
-        tout(count - 2, spread[0])
-        across(turned[1], spread[1])
-        tout(count - 1, spread[1])
+        tout(count - 2, 0)
+        across(count - 1, 1)
+        tout(count - 1, 1)
+
+
+def row_split(levels):
+    return (len(row_items(levels[:-1])) + 1) // 2
+
+
+def column_split(levels):
+    return (len(column_blocks(levels[:-1])) + 1) // 2
 
 
 def row_items(levels):
@@ -155,18 +161,24 @@
 def coarse_levels(mesh_shape, levels, *refs):
     count = len(levels)
     inputs, refs = refs[:count], refs[count:]
-    low_out, detail_out, refs = refs[0], refs[1], refs[2:]
+    low_out, mixed_out, rough_out, refs = refs[0], refs[1], refs[2], refs[3:]
     lows, refs = list(refs[: count - 2]) + [low_out], refs[count - 2 :]
-    details, refs = list(refs[: count - 2]) + [detail_out], refs[count - 2 :]
+    details, refs = refs[: count - 2], refs[count - 2 :]
+    outer, refs = refs[0], refs[1:]
     tops, bottoms, refs = refs[:count], refs[count : 2 * count], refs[2 * count :]
-    joined, turned_a, turned_b, spread_a, spread_b, *refs = refs
+    joined, smooth_a, smooth_b, rough_a, rough_b, spread_a, spread_b, *refs = refs
+    strip, tall_a, tall_b, *refs = refs
     send_top, send_bottom, below, above, *refs = refs
     send_first, send_last, from_right, from_left, *refs = refs
     corner_top, corner_bottom, down_right, down_left, up_right, up_left, *refs = refs
     edge_sem, body_sem, send_sem, recv_sem = refs
 
     def band(a, b):
-        return lows[0] if a == 0 else details[a - 1].at[b]
+        if a == 0:
+            return lows[0]
+        if a < count - 1:
+            return details[a - 1].at[b]
+        return mixed_out if b == 1 else outer.at[b // 2]
 
     n_rows, n_cols = mesh_shape
     row, col = lax.axis_index("rows"), lax.axis_index("cols")
@@ -192,12 +204,15 @@
 
     def load_tile(a, c, sem, into):
         n, h, w = levels[a]
-        src = inputs[a].at[:, :, pl.ds(c * LANES, LANES)]
+        columns = pl.ds(c * LANES, LANES)
+        rows = pl.ds(SUB, h)
         if a == 0:
-            dst = lows[0].at[pl.ds(c, 1), pl.ds(SUB, h), :]
+            load(inputs[a].at[:, :, columns], lows[0].at[pl.ds(c, 1), rows, :], sem, into)
+        elif a < count - 1:
+            load(inputs[a].at[:, :, columns], details[a - 1].at[:, c, rows, :], sem, into)
         else:
-            dst = details[a - 1].at[:, c, pl.ds(SUB, h), :]
-        load(src, dst, sem, into)
+            for b in range(n):
+                load(inputs[a].at[b, :, columns], band(a, b).at[c, rows, :], sem, into)
 
     for a in reversed(range(count)):
         n, h, w = levels[a]
@@ -257,8 +272,15 @@
         copy.start()
         sends.append(copy)
 
-    send(send_top, below, (row_prev, col))
-    send(send_bottom, above, (row_next, col))
+    few_pairs = row_split(levels)
+    rest_pairs = (len(items) + 1) // 2 - few_pairs
+
+    def send_rows(start, length):
+        part = pl.ds(start, length)
+        send(send_top.at[part], below.at[part], (row_prev, col))
+        send(send_bottom.at[part], above.at[part], (row_next, col))
+
+    send_rows(0, few_pairs)
     send(corner_top, down_right, (row_prev, col_prev))
     send(corner_top, down_left, (row_prev, col_next))
     send(corner_bottom, up_right, (row_next, col_prev))
@@ -290,15 +312,51 @@
         two = turned[min(2 * k + 1, len(blocks) - 1)]
         send_first[k] = jnp.where(upper, one[0], pltpu.roll(two[0], 4, 0))
         send_last[k] = jnp.where(upper, pltpu.roll(two[1], 4, 0), one[1])
-    send(send_first, from_right, (row, col_prev))
-    send(send_last, from_left, (row, col_next))
+    few_blocks = column_split(levels)
+    rest_blocks = (len(blocks) + 1) // 2 - few_blocks
+
+    def send_columns(start, length):
+        part = pl.ds(start, length)
+        send(send_first.at[part], from_right.at[part], (row, col_prev))
+        send(send_last.at[part], from_left.at[part], (row, col_next))
+
+    send_columns(0, few_blocks)
+    early = len(sends)
+    send_rows(few_pairs, rest_pairs)
+    send_columns(few_blocks, rest_blocks)
 
     for copy in bodies:
         copy.wait()
-    for copy in sends:
-        copy.wait()
-
-    for k in range((len(items) + 1) // 2):
+
+    n, h, w = levels[-1]
+    tiles = w // LANES
+    steps = (h + SUB) // SUB
+    last = 2 * h // LANES - 1
+
+    def turn_tall(tall, c, ks):
+        for k in ks:
+            rough_out[k, block(SUB + LANES * c), :] = tall[block(SUB + LANES * k), :].T
+
+    def turn_strips(c):
+        for i, (k, first) in enumerate(((0, 0), (last, h + SUB - STRIP))):
+            vertical(outer.at[0, c], outer.at[1, c], strip.at[i], STRIP // SUB, 1, 4 + first)
+            rough_out[k, block(SUB + LANES * c), :] = strip[i, pl.ds(SUB, LANES), :].T
+
+    inner = range(1, last)
+    vertical(outer.at[0, 0], outer.at[1, 0], tall_a, steps, 1)
+
+    def two_tiles(m, carry):
+        c = 2 * m
+        turn_tall(tall_a, c, inner)
+        vertical(outer.at[0, c + 1], outer.at[1, c + 1], tall_b, steps, 1)
+        after = jnp.minimum(c + 2, tiles - 1)
+        turn_tall(tall_b, c + 1, inner)
+        vertical(outer.at[0, after], outer.at[1, after], tall_a, steps, 1)
+        return carry
+
+    lax.fori_loop(0, tiles // 2, two_tiles, 0)
+
+    def unpack_rows(k):
         for i, (a, b, c) in enumerate(items[2 * k : 2 * k + 2]):
             h = levels[a][1]
             after, before = below[k], above[k]
@@ -306,7 +364,8 @@
                 after, before = pltpu.roll(after, 4, 0), pltpu.roll(before, 4, 0)
             band(a, b)[c, pl.ds(SUB + h, SUB), :] = after
             band(a, b)[c, pl.ds(0, SUB), :] = before
-    for k in range((len(blocks) + 1) // 2):
+
+    def unpack_columns(k):
         for i, parts in enumerate(blocks[2 * k : 2 * k + 2]):
             after, before = from_right[k], from_left[k]
             if i:
@@ -320,6 +379,13 @@
                     place : place + length
                 ]
                 place += length
+
+    for copy in sends[:early]:
+        copy.wait()
+    for k in range(few_pairs):
+        unpack_rows(k)
+    for k in range(few_blocks):
+        unpack_columns(k)
     right_side = lax.rem(lane, 8) < 4
     corner = jnp.where(
         upper,
@@ -342,36 +408,57 @@
                 smooth = low.at[c] if half == 0 else detail.at[0, c]
                 rough = detail.at[1, c] if half == 0 else detail.at[2, c]
                 out = joined.at[half, c]
-                vertical(smooth, rough, out, h, half)
+                vertical(smooth, rough, out, (h + SUB) // SUB, half)
                 out[pl.ds(SUB + 2 * h + LANES - SUB, SUB), :] = out[pl.ds(0, SUB), :]
             return carry
 
         lax.fori_loop(0, tiles + 1, columns, 0)
-
-        def tin(k, turned):
-            turn_in(joined, turned, k, tiles)
-
-        def across(turned, spread):
-            horizontal(turned, spread, w, True)
-
-        def tout(k, spread):
+        smooths, roughs, spreads = (smooth_a, smooth_b), (rough_a, rough_b), (spread_a, spread_b)
+
+        def tin(k, slot):
+            turn_in(joined.at[0], smooths[slot], k, tiles)
+            turn_in(joined.at[1], roughs[slot], k, tiles)
+
+        def across(k, slot):
+            horizontal(smooths[slot], roughs[slot], spreads[slot], w, True)
+
+        def tout(k, slot):
             for j in range(2 * tiles + 1):
-                target[j, block(SUB + LANES * k), :] = spread[pl.ds(SUB + LANES * j, LANES), :].T
-
-        blocks_of(2 * h // LANES + 1, tin, across, tout, (turned_a, turned_b), (spread_a, spread_b))
+                target[j, block(SUB + LANES * k), :] = spreads[slot][
+                    pl.ds(SUB + LANES * j, LANES), :
+                ].T
+
+        blocks_of(2 * h // LANES + 1, tin, across, tout)
         for j in range(2 * tiles + 1):
             target[j, pl.ds(0, SUB), :] = target[j, pl.ds(SUB + 2 * h + LANES - SUB, SUB), :]
 
-
-def finest_level(height, width, low, detail, out, joined, *refs):
-    turned_a, turned_b, spread_a, spread_b, finished, store_sem = refs
+    for copy in sends[early:]:
+        copy.wait()
+    for k in range(rest_pairs):
+        unpack_rows(few_pairs + k)
+    for k in range(rest_blocks):
+        unpack_columns(few_blocks + k)
+    n, h, w = levels[-1]
+    tiles = w // LANES
+
+    def border(c, carry):
+        turn_strips(c)
+        return carry
+
+    vertical(outer.at[0, tiles], outer.at[1, tiles], tall_a, steps, 1)
+    lax.fori_loop(0, tiles, border, 0)
+    turn_tall(tall_a, tiles, range(last + 1))
+    for k in range(last + 1):
+        wrap_around(rough_out.at[k], tiles)
+
+
+def finest_level(height, width, low, mixed, rough, out, joined, *refs):
+    smooth_a, smooth_b, spread_a, spread_b, finished, store_sem = refs
+    smooths, spreads = (smooth_a, smooth_b), (spread_a, spread_b)
     tiles = width // LANES
 
     def columns(c, carry):
-        for half in range(2):
-            smooth = low.at[c] if half == 0 else detail.at[0, c]
-            rough = detail.at[1, c] if half == 0 else detail.at[2, c]
-            vertical(smooth, rough, joined.at[half, c], height, half)
+        vertical(low.at[c], mixed.at[c], joined.at[c], (height + SUB) // SUB, 0)
         return carry
 
     lax.fori_loop(0, tiles + 1, columns, 0)
@@ -382,19 +469,19 @@
             finished.at[j, rows, :], out.at[rows, pl.ds(j * LANES, LANES)], store_sem.at[k, j]
         )
 
-    def tin(k, turned):
-        turn_in(joined, turned, k, tiles)
-
-    def across(turned, spread):
-        horizontal(turned, spread, width, False)
-
-    def tout(k, spread):
+    def tin(k, slot):
+        turn_in(joined, smooths[slot], k, tiles)
+
+    def across(k, slot):
+        horizontal(smooths[slot], rough.at[k], spreads[slot], width, False)
+
+    def tout(k, slot):
         for j in range(2 * tiles):
-            finished[j, block(LANES * k), :] = spread[pl.ds(SUB + LANES * j, LANES), :].T
+            finished[j, block(LANES * k), :] = spreads[slot][pl.ds(SUB + LANES * j, LANES), :].T
             store_copy(k, j).start()
 
     count = 2 * height // LANES
-    blocks_of(count, tin, across, tout, (turned_a, turned_b), (spread_a, spread_b))
+    blocks_of(count, tin, across, tout)
     for k in range(count):
         for j in range(2 * tiles):
             store_copy(k, j).wait()
@@ -411,31 +498,38 @@
     in_vmem = pl.BlockSpec(memory_space=pltpu.VMEM)
     n_pairs = (len(row_items(levels)) + 1) // 2
     n_blocks = (len(column_blocks(levels)) + 1) // 2
-    n_edges = sum(2 + len({0, w // LANES - 1}) for n, h, w in levels)
-    n_bodies = sum(max(w // LANES - 2, 0) for n, h, w in levels)
+    n_edges = sum(2 + len({0, w // LANES - 1}) for n, h, w in levels) + 4
+    n_bodies = 3 * sum(max(w // LANES - 2, 0) for n, h, w in levels)
     n, h, w = levels[-2]
     low_shape = lambda h, w: (w // LANES + 1, SUB + h + LANES, LANES)
     detail_shape = lambda h, w: (3, w // LANES + 1, h + 2 * SUB, LANES)
     _, height, width = levels[-1]
-    low, detail = pl.pallas_call(
+    low, mixed, rough = pl.pallas_call(
         functools.partial(coarse_levels, mesh_shape, levels),
-        out_shape=[vmem(*low_shape(height, width)), vmem(*detail_shape(height, width))],
+        out_shape=[
+            vmem(*low_shape(height, width)),
+            vmem(width // LANES + 1, height + 2 * SUB, LANES),
+            vmem(2 * height // LANES, SUB + width + LANES, LANES),
+        ],
         in_specs=[anywhere] * count,
-        out_specs=[in_vmem] * 2,
+        out_specs=[in_vmem] * 3,
         scratch_shapes=[vmem(*low_shape(h, w)) for _, h, w in levels[1:-1]]
         + [vmem(*detail_shape(h, w)) for _, h, w in levels[1:-1]]
+        + [vmem(2, width // LANES + 1, height + 2 * SUB, LANES)]
         + [vmem(b, SUB, w) for b, h, w in levels] * 2
         + [vmem(2, w // LANES + 1, SUB + 2 * h + LANES, LANES)]
-        + [vmem(2, SUB + w + LANES, LANES)] * 2
+        + [vmem(SUB + w + LANES, LANES)] * 4
         + [vmem(SUB + 2 * w + LANES, LANES)] * 2
+        + [vmem(2, 2 * STRIP, LANES)]
+        + [vmem(2 * height + 2 * SUB, LANES)] * 2
         + [vmem(n_pairs, SUB, LANES)] * 4
         + [vmem(n_blocks, SUB, LANES)] * 4
         + [vmem(SUB, LANES)] * 6
         + [
             pltpu.SemaphoreType.DMA((n_edges,)),
             pltpu.SemaphoreType.DMA((max(n_bodies, 1),)),
-            pltpu.SemaphoreType.DMA((8,)),
-            pltpu.SemaphoreType.DMA((8,)),
+            pltpu.SemaphoreType.DMA((12,)),
+            pltpu.SemaphoreType.DMA((12,)),
         ],
         compiler_params=pltpu.CompilerParams(
             collective_id=0, has_side_effects=True, vmem_limit_bytes=40 * 1024 * 1024
@@ -447,10 +541,10 @@
     return pl.pallas_call(
         functools.partial(finest_level, height, width),
         out_shape=jax.ShapeDtypeStruct((2 * height, 2 * width), f32),
-        in_specs=[in_vmem] * 2,
+        in_specs=[in_vmem] * 3,
         out_specs=anywhere,
-        scratch_shapes=[vmem(2, tiles + 1, 2 * height + 2 * SUB, LANES)]
-        + [vmem(2, SUB + width + LANES, LANES)] * 2
+        scratch_shapes=[vmem(tiles + 1, 2 * height + 2 * SUB, LANES)]
+        + [vmem(SUB + width + LANES, LANES)] * 2
         + [vmem(2 * width + 2 * SUB, LANES)] * 2
         + [
             vmem(2 * tiles, 2 * height, LANES),
@@ -458,7 +552,7 @@
         ],
         compiler_params=pltpu.CompilerParams(vmem_limit_bytes=40 * 1024 * 1024),
         name="finest_level",
-    )(low, detail)
+    )(low, mixed, rough)
 
 
 def solution(mesh):

time: 26.6 us -> 25.9 us (0.974)
  Pallas kernels: 26.5 us -> 25.8 us
    pallas_call x1, Pallas kernels: 9.81 us -> 7.8 us  [per_device(): pl.pallas_call(functools.partial(finest_level, height, width), out_shape=...]
    pallas_call x1, Pallas kernels: 16.7 us -> 18 us  [per_device(): pl.pallas_call(functools.partial(coarse_levels, mesh_shape, levels), out_...]
where the time goes in v2:
time: 25.9 us; the launch traced here: 25.8 us
  Pallas kernels  25.8 us (100%)
    pallas_call x1, Pallas kernels, per_device(): pl.pallas_call(functools.partial(coarse_levels, mesh_shape, levels), out_...  18 us
    pallas_call x1, Pallas kernels, per_device(): pl.pallas_call(functools.partial(finest_level, height, width), out_shape=...  7.8 us

profile of v2, /device:TPU:0, one launch (start us, length us, event | category | flops | bytes accessed | tf_op | source)
XLA Modules:
  0.0 25.8 jit_solution(6772456046330178649)
XLA Ops:
  0.0 18.0 %coarse_levels.1 = (f32[9,648,128]{2,1,0:T(8,128)S(1)}, f32[9,528,128]{2,1,0:T(8,128)S(1)}, f32[8,1160,128]{2,1,0:T(8,128)S(1)}) custom-call(f32[1,64,128]{2,1,0:T(8,128)} %bitcast.1, f32[3,64,128]{2,1,0:T(8,128)} %refs_1_.1, f32[3,128,256]{2,1,0:T(8,128)} %refs_2_.1, f32[3,256,512]{2,1,0:T(8,128)} %refs_3_.1, f32[3,512,1024]{2,1,0:T(8,128)} %refs_4_.1), custom_call_target="tpu_custom_call" | custom-call | tf_op jit(solution)/shard_map/coarse_levels/pallas_call | solution.py:507
  18.0 7.8 %finest_level.1 = f32[1024,2048]{1,0:T(8,128)} custom-call(f32[9,648,128]{2,1,0:T(8,128)S(1)} %get-tuple-element.8.low, f32[9,528,128]{2,1,0:T(8,128)S(1)} %get-tuple-element.9.mixed, f32[8,1160,128]{2,1,0:T(8,128)S(1)} %get-tuple-element.10.rough), custom_call_target="tpu_custom_call" | custom-call | tf_op jit(solution)/shard_map/finest_level/pallas_call | solution.py:541

commit v3 on v2

--- a/solution.py
+++ b/solution.py
@@ -17,6 +17,7 @@
 LANES = 128
 SUB = 8
 STRIP = 72
+GROUP = 4
 BIG, SMALL = lift_scale * lift_scale, 1.0 / (lift_scale * lift_scale)
 
 
@@ -95,41 +96,60 @@
         spread[pl.ds(SUB + 2 * width + LANES - SUB, SUB), :] = spread[pl.ds(0, SUB), :]
 
 
-def turn_in(joined, turned, k, tiles):
-    for c in range(tiles + 1):
-        turned[pl.ds(SUB + LANES * c, LANES), :] = joined[c, block(SUB + LANES * k), :].T
-    wrap_around(turned, tiles)
+def turn(tall, turned, c, ks):
+    for k in ks:
+        turned[k, block(SUB + LANES * c), :] = tall[block(SUB + LANES * k), :].T
 
 
 def wrap_around(turned, tiles):
     turned[pl.ds(0, SUB), :] = turned[pl.ds(SUB + LANES * tiles + LANES - SUB, SUB), :]
 
 
-def blocks_of(count, tin, across, tout):
-    tin(0, 0)
+def repeat(count, body):
+    if count == 1:
+        body(0, 0)
+    elif count:
+        lax.fori_loop(0, count, body, 0)
+
+
+def tiles_of(tiles, down, across):
+    down(0, 0)
+
+    def two(m, carry):
+        c = 2 * m
+        across(c, 0)
+        down(c + 1, 1)
+        across(c + 1, 1)
+        down(c + 2, 0)
+        return carry
+
+    repeat(tiles // 2, two)
+    if tiles % 2:
+        across(tiles - 1, 0)
+        down(tiles, 1)
+        across(tiles, 1)
+    else:
+        across(tiles, 0)
+
+
+def blocks_of(count, across, out):
     across(0, 0)
-    if count > 1:
-        tin(1, 1)
-    pairs = (count - 1) // 2
 
     def two(m, carry):
         k = 2 * m
-        tout(k, 0)
+        out(k, 0)
         across(k + 1, 1)
-        tin(k + 2, 0)
-        tout(k + 1, 1)
+        out(k + 1, 1)
         across(k + 2, 0)
-        tin(jnp.minimum(k + 3, count - 1), 1)
         return carry
 
-    if pairs:
-        lax.fori_loop(0, pairs, two, 0)
+    repeat((count - 1) // 2, two)
     if count % 2:
-        tout(count - 1, 0)
+        out(count - 1, 0)
     else:
-        tout(count - 2, 0)
+        out(count - 2, 0)
         across(count - 1, 1)
-        tout(count - 1, 1)
+        out(count - 1, 1)
 
 
 def row_split(levels):
@@ -166,8 +186,8 @@
     details, refs = refs[: count - 2], refs[count - 2 :]
     outer, refs = refs[0], refs[1:]
     tops, bottoms, refs = refs[:count], refs[count : 2 * count], refs[2 * count :]
-    joined, smooth_a, smooth_b, rough_a, rough_b, spread_a, spread_b, *refs = refs
-    strip, tall_a, tall_b, *refs = refs
+    smooth_turned, rough_turned, strip, *refs = refs
+    spreads, smooth_talls, rough_talls, refs = refs[:2], refs[2:4], refs[4:6], refs[6:]
     send_top, send_bottom, below, above, *refs = refs
     send_first, send_last, from_right, from_left, *refs = refs
     corner_top, corner_bottom, down_right, down_left, up_right, up_left, *refs = refs
@@ -333,25 +353,19 @@
     steps = (h + SUB) // SUB
     last = 2 * h // LANES - 1
 
-    def turn_tall(tall, c, ks):
-        for k in ks:
-            rough_out[k, block(SUB + LANES * c), :] = tall[block(SUB + LANES * k), :].T
-
-    def turn_strips(c):
-        for i, (k, first) in enumerate(((0, 0), (last, h + SUB - STRIP))):
-            vertical(outer.at[0, c], outer.at[1, c], strip.at[i], STRIP // SUB, 1, 4 + first)
-            rough_out[k, block(SUB + LANES * c), :] = strip[i, pl.ds(SUB, LANES), :].T
-
     inner = range(1, last)
-    vertical(outer.at[0, 0], outer.at[1, 0], tall_a, steps, 1)
+
+    def down(c, slot):
+        vertical(outer.at[0, c], outer.at[1, c], rough_talls[slot], steps, 1)
+
+    down(0, 0)
 
     def two_tiles(m, carry):
         c = 2 * m
-        turn_tall(tall_a, c, inner)
-        vertical(outer.at[0, c + 1], outer.at[1, c + 1], tall_b, steps, 1)
-        after = jnp.minimum(c + 2, tiles - 1)
-        turn_tall(tall_b, c + 1, inner)
-        vertical(outer.at[0, after], outer.at[1, after], tall_a, steps, 1)
+        turn(rough_talls[0], rough_out, c, inner)
+        down(c + 1, 1)
+        turn(rough_talls[1], rough_out, c + 1, inner)
+        down(c + 2, 0)
         return carry
 
     lax.fori_loop(0, tiles // 2, two_tiles, 0)
@@ -403,24 +417,26 @@
         tiles = w // LANES
         low, detail, target = lows[level], details[level], lows[level + 1]
 
-        def columns(c, carry):
-            for half in range(2):
+        count_k = 2 * h // LANES + 1
+
+        def down(c, slot):
+            for half, tall in enumerate((smooth_talls[slot], rough_talls[slot])):
                 smooth = low.at[c] if half == 0 else detail.at[0, c]
                 rough = detail.at[1, c] if half == 0 else detail.at[2, c]
-                out = joined.at[half, c]
-                vertical(smooth, rough, out, (h + SUB) // SUB, half)
-                out[pl.ds(SUB + 2 * h + LANES - SUB, SUB), :] = out[pl.ds(0, SUB), :]
-            return carry
-
-        lax.fori_loop(0, tiles + 1, columns, 0)
-        smooths, roughs, spreads = (smooth_a, smooth_b), (rough_a, rough_b), (spread_a, spread_b)
-
-        def tin(k, slot):
-            turn_in(joined.at[0], smooths[slot], k, tiles)
-            turn_in(joined.at[1], roughs[slot], k, tiles)
-
-        def across(k, slot):
-            horizontal(smooths[slot], roughs[slot], spreads[slot], w, True)
+                vertical(smooth, rough, tall, (h + SUB) // SUB, half)
+                tall[pl.ds(SUB + 2 * h + LANES - SUB, SUB), :] = tall[pl.ds(0, SUB), :]
+
+        def across(c, slot):
+            turn(smooth_talls[slot], smooth_turned, c, range(count_k))
+            turn(rough_talls[slot], rough_turned, c, range(count_k))
+
+        tiles_of(tiles, down, across)
+        for k in range(count_k):
+            wrap_around(smooth_turned.at[k], tiles)
+            wrap_around(rough_turned.at[k], tiles)
+
+        def lift_columns(k, slot):
+            horizontal(smooth_turned.at[k], rough_turned.at[k], spreads[slot], w, True)
 
         def tout(k, slot):
             for j in range(2 * tiles + 1):
@@ -428,7 +444,7 @@
                     pl.ds(SUB + LANES * j, LANES), :
                 ].T
 
-        blocks_of(2 * h // LANES + 1, tin, across, tout)
+        blocks_of(count_k, lift_columns, tout)
         for j in range(2 * tiles + 1):
             target[j, pl.ds(0, SUB), :] = target[j, pl.ds(SUB + 2 * h + LANES - SUB, SUB), :]
 
@@ -441,50 +457,58 @@
     n, h, w = levels[-1]
     tiles = w // LANES
 
-    def border(c, carry):
-        turn_strips(c)
+    vertical(outer.at[0, tiles], outer.at[1, tiles], rough_talls[0], steps, 1)
+    turn(rough_talls[0], rough_out, tiles, range(last + 1))
+
+    def border(m, carry):
+        for u in range(GROUP):
+            c = GROUP * m + u
+            for i, first in enumerate((4, 4 + h + SUB - STRIP)):
+                vertical(outer.at[0, c], outer.at[1, c], strip.at[u, i], STRIP // SUB, 1, first)
+        for u in range(GROUP):
+            c = GROUP * m + u
+            for i, k in enumerate((0, last)):
+                rough_out[k, block(SUB + LANES * c), :] = strip[u, i, pl.ds(SUB, LANES), :].T
         return carry
 
-    vertical(outer.at[0, tiles], outer.at[1, tiles], tall_a, steps, 1)
-    lax.fori_loop(0, tiles, border, 0)
-    turn_tall(tall_a, tiles, range(last + 1))
+    repeat(tiles // GROUP, border)
     for k in range(last + 1):
         wrap_around(rough_out.at[k], tiles)
 
 
-def finest_level(height, width, low, mixed, rough, out, joined, *refs):
-    smooth_a, smooth_b, spread_a, spread_b, finished, store_sem = refs
-    smooths, spreads = (smooth_a, smooth_b), (spread_a, spread_b)
+def finest_level(height, width, low, mixed, rough, out, *refs):
+    tall_a, tall_b, turned, spread_a, spread_b, finished, store_sem = refs
+    talls, spreads = (tall_a, tall_b), (spread_a, spread_b)
     tiles = width // LANES
-
-    def columns(c, carry):
-        vertical(low.at[c], mixed.at[c], joined.at[c], (height + SUB) // SUB, 0)
-        return carry
-
-    lax.fori_loop(0, tiles + 1, columns, 0)
-
-    def store_copy(k, j):
+    count = 2 * height // LANES
+
+    def down(c, slot):
+        vertical(low.at[c], mixed.at[c], talls[slot], (height + SUB) // SUB, 0)
+
+    def across(c, slot):
+        turn(talls[slot], turned, c, range(count))
+
+    tiles_of(tiles, down, across)
+    for k in range(count):
+        wrap_around(turned.at[k], tiles)
+
+    def store_copy(k):
         rows = block(LANES * k)
-        return pltpu.make_async_copy(
-            finished.at[j, rows, :], out.at[rows, pl.ds(j * LANES, LANES)], store_sem.at[k, j]
-        )
-
-    def tin(k, slot):
-        turn_in(joined, smooths[slot], k, tiles)
-
-    def across(k, slot):
-        horizontal(smooths[slot], rough.at[k], spreads[slot], width, False)
+        return pltpu.make_async_copy(finished.at[rows, :], out.at[rows, :], store_sem.at[k])
+
+    def lift_columns(k, slot):
+        horizontal(turned.at[k], rough.at[k], spreads[slot], width, False)
 
     def tout(k, slot):
         for j in range(2 * tiles):
-            finished[j, block(LANES * k), :] = spreads[slot][pl.ds(SUB + LANES * j, LANES), :].T
-            store_copy(k, j).start()
-
-    count = 2 * height // LANES
-    blocks_of(count, tin, across, tout)
+            finished[block(LANES * k), pl.ds(LANES * j, LANES)] = spreads[slot][
+                pl.ds(SUB + LANES * j, LANES), :
+            ].T
+        store_copy(k).start()
+
+    blocks_of(count, lift_columns, tout)
     for k in range(count):
-        for j in range(2 * tiles):
-            store_copy(k, j).wait()
+        store_copy(k).wait()
 
 
 def per_device(mesh_shape, coarse, *details):
@@ -517,11 +541,10 @@
         + [vmem(*detail_shape(h, w)) for _, h, w in levels[1:-1]]
         + [vmem(2, width // LANES + 1, height + 2 * SUB, LANES)]
         + [vmem(b, SUB, w) for b, h, w in levels] * 2
-        + [vmem(2, w // LANES + 1, SUB + 2 * h + LANES, LANES)]
-        + [vmem(SUB + w + LANES, LANES)] * 4
+        + [vmem(2 * h // LANES + 1, SUB + w + LANES, LANES)] * 2
+        + [vmem(GROUP, 2, 2 * STRIP, LANES)]
         + [vmem(SUB + 2 * w + LANES, LANES)] * 2
-        + [vmem(2, 2 * STRIP, LANES)]
-        + [vmem(2 * height + 2 * SUB, LANES)] * 2
+        + [vmem(2 * height + 2 * SUB, LANES)] * 4
         + [vmem(n_pairs, SUB, LANES)] * 4
         + [vmem(n_blocks, SUB, LANES)] * 4
         + [vmem(SUB, LANES)] * 6
@@ -543,12 +566,12 @@
         out_shape=jax.ShapeDtypeStruct((2 * height, 2 * width), f32),
         in_specs=[in_vmem] * 3,
         out_specs=anywhere,
-        scratch_shapes=[vmem(tiles + 1, 2 * height + 2 * SUB, LANES)]
-        + [vmem(SUB + width + LANES, LANES)] * 2
+        scratch_shapes=[vmem(2 * height + 2 * SUB, LANES)] * 2
+        + [vmem(2 * height // LANES, SUB + width + LANES, LANES)]
         + [vmem(2 * width + 2 * SUB, LANES)] * 2
         + [
-            vmem(2 * tiles, 2 * height, LANES),
-            pltpu.SemaphoreType.DMA((2 * height // LANES, 2 * tiles)),
+            vmem(2 * height, 2 * width),
+            pltpu.SemaphoreType.DMA((2 * height // LANES,)),
         ],
         compiler_params=pltpu.CompilerParams(vmem_limit_bytes=40 * 1024 * 1024),
         name="finest_level",

time: 25.9 us -> 23.7 us (0.915)
  Pallas kernels: 25.8 us -> 23.5 us
    pallas_call x1, Pallas kernels: 18 us -> 16.5 us  [per_device(): pl.pallas_call(functools.partial(coarse_levels, mesh_shape, levels), out_...]
    pallas_call x1, Pallas kernels: 7.8 us -> 7.01 us  [per_device(): pl.pallas_call(functools.partial(finest_level, height, width), out_shape=...]
where the time goes in v3:
time: 23.7 us; the launch traced here: 23.6 us
  Pallas kernels  23.5 us (99%)
    pallas_call x1, Pallas kernels, per_device(): pl.pallas_call(functools.partial(coarse_levels, mesh_shape, levels), out_...  16.5 us
    pallas_call x1, Pallas kernels, per_device(): pl.pallas_call(functools.partial(finest_level, height, width), out_shape=...  7.01 us

profile of v3, /device:TPU:0, one launch (start us, length us, event | category | flops | bytes accessed | tf_op | source)
XLA Modules:
  0.0 23.6 jit_solution(8548299791676378966)
XLA Ops:
  0.0 16.5 %coarse_levels.1 = (f32[9,648,128]{2,1,0:T(8,128)S(1)}, f32[9,528,128]{2,1,0:T(8,128)S(1)}, f32[8,1160,128]{2,1,0:T(8,128)S(1)}) custom-call(f32[1,64,128]{2,1,0:T(8,128)} %bitcast.1, f32[3,64,128]{2,1,0:T(8,128)} %refs_1_.1, f32[3,128,256]{2,1,0:T(8,128)} %refs_2_.1, f32[3,256,512]{2,1,0:T(8,128)} %refs_3_.1, f32[3,512,1024]{2,1,0:T(8,128)} %refs_4_.1), custom_call_target="tpu_custom_call" | custom-call | tf_op jit(solution)/shard_map/coarse_levels/pallas_call | solution.py:531
  16.5 7.0 %finest_level.1 = f32[1024,2048]{1,0:T(8,128)} custom-call(f32[9,648,128]{2,1,0:T(8,128)S(1)} %get-tuple-element.8.low, f32[9,528,128]{2,1,0:T(8,128)S(1)} %get-tuple-element.9.mixed, f32[8,1160,128]{2,1,0:T(8,128)S(1)} %get-tuple-element.10.rough), custom_call_target="tpu_custom_call" | custom-call | tf_op jit(solution)/shard_map/finest_level/pallas_call | solution.py:564
